TPU v7x, 256 devices: a whole 4x4x8 slice. The times are simulated.
256 devices in a mesh: tm: 2 (over y_lo), row: 16 (over y_hi, z), col: 8 (over x, core).
Axes of the slice: x: 4, y: 4 (y_hi: 2, y_lo: 2; y = y_hi * 2 + y_lo), z: 8, core: 2. Of those that a mesh axis runs over, the one named last changes fastest.
Arguments:
- returns: bfloat16 [272, 16384], P('tm', ('row', 'col')), may hold values from -60 to 60
- window: int32 [1], replicated, may hold values from 200 to 256
- out_days: int32 [4], replicated, may hold values from 255 to 271
Outputs:
- correlation: bfloat16 [4, 16384, 16384], P(None, 'row', ('col', 'tm'))
Inputs may be any that keep to these rules, and one draw needn't show every extreme that they name: One window length for all days. `out_days`: days may repeat.
All inputs are finite; a program needn't handle non-finite values.
Results may differ from a plain program's by a relative error of at most 0.001.
Values may be sent and summed in bfloat16 or wider, within the bound.
No kernel may reach another device: no remote copies, remote signals or barrier semaphores. Data moves between devices by JAX's collectives and lax.ppermute only.
A program may use at most 128 MiB of HBM per device.

v0:
```python
import jax
import jax.numpy as jnp
from jax import lax
from jax.sharding import PartitionSpec as P


def moments(mask, block):
    series = block.astype(jnp.float32)
    first = jnp.dot(mask, series, precision=lax.Precision.HIGHEST)
    second = jnp.dot(mask, series * series, precision=lax.Precision.HIGHEST)
    return (first, second)


def on_device(returns, window, out_days):
    width = window[0]
    wide = width.astype(jnp.float32)
    tm_count = lax.axis_size("tm")
    tm_index = lax.axis_index("tm")
    share = lax.axis_size("row") // lax.axis_size("col")
    local = lax.all_gather(returns, "tm", axis=0, tiled=True)
    row_series = lax.all_gather(local, "col", axis=1, tiled=True)
    block_width = row_series.shape[1]
    col_index = lax.axis_index("col")
    range_width = share * block_width
    half = range_width // tm_count
    half_start = tm_index * half
    range_start = col_index * range_width
    wanted_start = range_start + half_start
    everything = lax.all_gather(row_series, "row", axis=1, tiled=True)
    col_series = lax.dynamic_slice_in_dim(everything, wanted_start, half, 1)
    day_count = local.shape[0]
    day_ids = jnp.arange(day_count, dtype=jnp.int32)
    inside = (day_ids[None, :] <= out_days[:, None]) & (
        day_ids[None, :] > out_days[:, None] - width
    )
    mask = jnp.where(inside, 1.0, 0.0).astype(jnp.float32)
    weighted = mask.astype(jnp.bfloat16)[:, :, None] * row_series[None, :, :]
    gram = jnp.einsum("kda,db->kab", weighted, col_series, preferred_element_type=jnp.float32)
    first_rows, second_rows = moments(mask, row_series)
    first_cols, second_cols = moments(mask, col_series)
    scale_rows = lax.rsqrt((second_rows - first_rows * first_rows / wide) / wide + 1e-06)
    scale_cols = lax.rsqrt((second_cols - first_cols * first_cols / wide) / wide + 1e-06)
    cov = gram - first_rows[:, :, None] * first_cols[:, None, :] / wide
    return (cov * scale_rows[:, :, None] * scale_cols[:, None, :] / wide).astype(jnp.bfloat16)


def solution(mesh):
    return jax.shard_map(
        on_device,
        mesh=mesh,
        in_specs=(P("tm", ("row", "col")), P(), P()),
        out_specs=P(None, "row", ("col", "tm")),
        check_vma=False,
    )
```

profile of v0, /device:TPU:1, one launch (start us, length us, event | category | flops | bytes accessed | tf_op | source)
XLA Modules:
  0.0 188.0 jit_solution(15276482759653825243)
XLA Ops:
  6.5 0.0 all-gather.2.cloned.1.call-start
  6.5 4.4 %all_gather.9 = bf16[272,128]{1,0:T(8,128)(2,1)S(1)} all-gather(bf16[136,128]{1,0:T(8,128)(2,1)} %param.3), channel_id=1, replica_groups=mesh['tm'=2,'row'=16,'col'=8] {'tm'}, dimensions={0}, use_global_device_ids=true | all-gather | bytes 104448 | tf_op jit(solution)/shard_map/all_gather | solution.py:20
  10.9 16.4 %all_gather.10 = bf16[272,1024]{1,0:T(8,128)(2,1)} all-gather(bf16[272,128]{1,0:T(8,128)(2,1)S(1)} %all_gather.9), channel_id=1, replica_groups=mesh['tm'=2,'row'=16,'col'=8] {'col'}, dimensions={1}, use_global_device_ids=true | all-gather | bytes 626688 | tf_op jit(solution)/shard_map/all_gather | solution.py:21
  27.3 0.0 all-gather.2.cloned.1.call-update
  28.0 0.7 broadcast_subtract_fusion
  28.7 0.7 select_convert_fusion
  29.4 1.4 fusion.41
  30.8 1.8 fusion.18
  32.7 135.3 %all-gather.2.cloned.1.call-done = bf16[272,16384]{1,0:T(8,128)(2,1)} async-done(((bf16[272,1024]{1,0:T(8,128)(2,1)}), bf16[272,16384]{1,0:T(8,128)(2,1)}) %all-gather.2.cloned.1.call-update) | async-done | bytes 8912912 | tf_op jit(solution)/shard_map/all_gather | solution.py:29
  168.0 1.4 fusion.35
  169.4 1.8 fusion.30
  171.2 9.9 %divide_convert_fusion = bf16[4,1024,1024]{2,1,0:T(8,128)(2,1)} fusion(f32[4,1024]{1,0:T(4,128)S(1)} %fusion.30, f32[4,1024]{1,0:T(4,128)S(1)} %fusion.18, f32[]{:T(128)S(6)} %convert_element_type.20, f32[4,1024]{1,0:T(4,128)S(1)} %fusion.35, f32[4,1024]{1,0:T(4,128)S(1)} %fusion.41, bf16[272,1024]{1,0:T(8,128)(2,1)} %all_gather.10, ...), kind=kOutput, calls=%fused_computation | convolution fusion | flops 2312175616 | bytes 9570440 | tf_op jit(solution)/shard_map/kda,db->kab/dot_general | solution.py:38
Async XLA Ops:
  6.5 161.4 %all-gather.2.cloned.1.call-start = ((), (), s32[]{:S(2)}) async-start(), calls=%async_computation | async-start | bytes 9469952 | tf_op jit(solution)/shard_map/all_gather | solution.py:29
Sparse Core Ops, SparseCore 0:
  27.5 140.4 all-gather.1
where the time goes:
time: 188 us
  waiting for transfers between devices  135 us (72%)
  blocking collectives  20.8 us (11%)
  matrix products  16.4 us (9%)
  between operations  14.1 us (8%)
    all_gather x1, waiting for transfers between devices, on_device(): everything = lax.all_gather(row_series, 'row', axis=1, tiled=True)  135 us
    all_gather x1, blocking collectives, on_device(): row_series = lax.all_gather(local, 'col', axis=1, tiled=True)  16.4 us
    dot_general x1, matrix products, on_device(): jnp.einsum('kda,db->kab', weighted, col_series, preferred_element_type=jn...  9.89 us
    all_gather x1, blocking collectives, on_device(): local = lax.all_gather(returns, 'tm', axis=0, tiled=True)  4.36 us
  transfers between devices with their start and end apart: 1, of which 1 were waited for; matrix products, arithmetic and copies ran while one was open for 2% of the time, Pallas kernels for 0%

commit v1 on v0

--- a/solution.py
+++ b/solution.py
@@ -26,7 +26,7 @@
     half_start = tm_index * half
     range_start = col_index * range_width
     wanted_start = range_start + half_start
-    everything = lax.all_gather(row_series, "row", axis=1, tiled=True)
+    everything = jnp.concatenate(lax.all_gather(row_series, "row"), axis=1)
     col_series = lax.dynamic_slice_in_dim(everything, wanted_start, half, 1)
     day_count = local.shape[0]
     day_ids = jnp.arange(day_count, dtype=jnp.int32)

time: 188 us -> 197 us (1.048)
  local copies, waits for them, and re-layouts: 0 us -> 8.58 us
    unnamed x0 -> x5, local copies, waits for them, and re-layouts: none -> 8.58 us
where the time goes in v1:
time: 197 us; the launch traced here: 196 us
  waiting for transfers between devices  135 us (69%)
  blocking collectives  20.8 us (11%)
  matrix products  16.3 us (8%)
  between operations  14.1 us (7%)
  local copies, waits for them, and re-layouts  8.58 us (4%)
    all_gather x1, waiting for transfers between devices, on_device(): everything = jnp.concatenate(lax.all_gather(row_series, 'row'), axis=1)  135 us
    all_gather x1, blocking collectives, on_device(): row_series = lax.all_gather(local, 'col', axis=1, tiled=True)  16.4 us
    dot_general x1, matrix products, on_device(): jnp.einsum('kda,db->kab', weighted, col_series, preferred_element_type=jn...  9.74 us
    unnamed x5, local copies, waits for them, and re-layouts  8.58 us
    all_gather x1, blocking collectives, on_device(): local = lax.all_gather(returns, 'tm', axis=0, tiled=True)  4.36 us
  transfers between devices with their start and end apart: 1, of which 1 were waited for; matrix products, arithmetic and copies ran while one was open for 2% of the time, Pallas kernels for 0%

profile of v1, /device:TPU:1, one launch (start us, length us, event | category | flops | bytes accessed | tf_op | source)
XLA Modules:
  0.0 196.4 jit_solution(16643541785082876352)
XLA Ops:
  6.5 0.0 all-gather.3.cloned.1.call-start
  6.5 4.4 %all_gather.10 = bf16[272,128]{1,0:T(8,128)(2,1)S(1)} all-gather(bf16[136,128]{1,0:T(8,128)(2,1)} %param.3), channel_id=1, replica_groups=mesh['tm'=2,'row'=16,'col'=8] {'tm'}, dimensions={0}, use_global_device_ids=true | all-gather | bytes 104448 | tf_op jit(solution)/shard_map/all_gather | solution.py:20
  10.9 16.4 %all_gather.11 = bf16[272,1024]{1,0:T(8,128)(2,1)} all-gather(bf16[272,128]{1,0:T(8,128)(2,1)S(1)} %all_gather.10), channel_id=1, replica_groups=mesh['tm'=2,'row'=16,'col'=8] {'col'}, dimensions={1}, use_global_device_ids=true | all-gather | bytes 626688 | tf_op jit(solution)/shard_map/all_gather | solution.py:21
  27.3 0.0 all-gather.3.cloned.1.call-update
  28.0 0.7 broadcast_subtract_fusion
  28.7 0.7 select_convert_fusion
  29.4 1.4 fusion.41
  30.8 1.8 fusion.18
  32.7 135.3 %all-gather.3.cloned.1.call-done = bf16[4352,1024]{1,0:T(8,128)(2,1)} async-done(((bf16[272,1024]{1,0:T(8,128)(2,1)}), bf16[4352,1024]{1,0:T(8,128)(2,1)}) %all-gather.3.cloned.1.call-update) | async-done | bytes 8912912 | tf_op jit(solution)/shard_map/all_gather | solution.py:29
  168.0 0.0 copy-start.1
  168.0 0.0 copy-start
  168.0 8.6 %copy.5 = bf16[34,8,16,1024]{3,1,2,0:T(8,128)(2,1)} copy(bf16[34,8,16,1024]{3,1,0,2:T(8,128)(2,1)} %bitcast.16) | data formatting | bytes 17825792
  176.5 0.0 copy-done.1
  176.5 1.4 fusion.35
  178.0 1.8 fusion.30
  179.8 0.0 copy-done
  179.8 9.7 %divide_convert_fusion = bf16[4,1024,1024]{2,1,0:T(8,128)(2,1)} fusion(f32[4,1024]{1,0:T(4,128)S(1)} %fusion.30, f32[4,1024]{1,0:T(4,128)S(1)} %fusion.18, f32[]{:T(128)S(6)} %convert_element_type.20, f32[4,1024]{1,0:T(4,128)S(1)} %fusion.35, f32[4,1024]{1,0:T(4,128)S(1)} %fusion.41, bf16[272,1024]{1,0:T(8,128)(2,1)S(1)} %copy-done, ...), kind=kOutput, calls=%fused_computation | convolution fusion | flops 2312175616 | bytes 9570440 | tf_op jit(solution)/shard_map/kda,db->kab/dot_general | solution.py:38
Async XLA Ops:
  6.5 161.4 %all-gather.3.cloned.1.call-start = ((), (), s32[]{:S(2)}) async-start(), calls=%async_computation | async-start | bytes 9469952 | tf_op jit(solution)/shard_map/all_gather | solution.py:29
  168.0 8.6 %copy-start.1 = (s32[4]{0:T(128)S(1)}, s32[4]{0:T(128)}, u32[]{:S(2)}) copy-start(s32[4]{0:T(128)} %param.5) | copy-start | bytes 52
  168.0 11.8 %copy-start = (bf16[272,1024]{1,0:T(8,128)(2,1)S(1)}, bf16[272,1024]{1,0:T(8,128)(2,1)}, u32[]{:S(2)}) copy-start(bf16[272,1024]{1,0:T(8,128)(2,1)} %all_gather.11) | copy-start | bytes 1671172
Sparse Core Ops, SparseCore 0:
  27.5 140.4 all-gather.2
